TPU v7x, 64 devices: a 2x2x8 block of a 4x4x8 slice. The times are simulated.
64 devices in a mesh: rep: 8 (over x, y, core), dp: 8 (over z).
Axes of the slice: x: 2, y: 2, z: 8, core: 2. Of those that a mesh axis runs over, the one named last changes fastest.
The devices are a block of a 4x4x8 slice.
Arguments:
- x: bfloat16 [64, 2048, 512], P(('rep', 'dp')), parts along dimension 0
- dy: bfloat16 [64, 2048, 512], P(('rep', 'dp')), parts along dimension 0
- w_gate: bfloat16 [2, 512, 1792], P(None, 'dp')
- w_up: bfloat16 [2, 512, 1792], P(None, 'dp')
- w_down: bfloat16 [2, 1792, 512], P(None, 'dp')
Outputs:
- output 1: bfloat16 [64, 2048, 512], P(('rep', 'dp')), parts along dimension 0
- output 2: bfloat16 [16, 512, 1792], P('rep', 'dp'), parts along dimension 0
- output 3: bfloat16 [16, 512, 1792], P('rep', 'dp'), parts along dimension 0
- output 4: bfloat16 [16, 1792, 512], P('rep', 'dp'), parts along dimension 0
There are 8 independent parts. A program takes and returns all parts, laid end to end along the dimension named above; an argument that names none is the same for every part.
All inputs are finite; a program needn't handle non-finite values.
Results may differ from a plain program's by a relative error of at most 0.018.
Values are sent between devices in bfloat16 or wider.
A program may use at most 768 MiB of HBM per device.

v0:
```python
import jax
import jax.numpy as jnp
from jax import lax

NAMES = ("w_gate", "w_up", "w_down")


def matmul(a, w):
    return jnp.dot(a, w, preferred_element_type=jnp.float32).astype(jnp.bfloat16)


def normed(h):
    wide = h.astype(jnp.float32)
    scale = lax.rsqrt(jnp.mean(wide**2, -1, keepdims=True) + 1e-6)
    return (wide * scale).astype(jnp.bfloat16)


def layer(h, w):
    a = normed(h)
    gate = jnp.dot(a, w["w_gate"], preferred_element_type=jnp.float32)
    up = jnp.dot(a, w["w_up"], preferred_element_type=jnp.float32)
    return h + matmul((jax.nn.silu(gate) * up).astype(jnp.bfloat16), w["w_down"])


def stack(weights, h):
    for number in range(weights["w_gate"].shape[0]):
        h = layer(h, {name: w[number] for name, w in weights.items()})
    return h


def solution(mesh):
    groups = mesh.shape["rep"]

    def step(x, dy, *weights):
        shape = x.shape
        x, dy = (t.reshape(groups, -1, *t.shape[1:]) for t in (x, dy))

        def of_a_group(x, dy):
            _, back = jax.vjp(stack, dict(zip(NAMES, weights, strict=True)), x)
            by_weights, by_x = back(dy)
            return (by_x, *(by_weights[name] for name in NAMES))

        by_x, *by_weights = jax.vmap(of_a_group)(x, dy)
        return (by_x.reshape(shape), *(t.reshape(-1, *t.shape[2:]) for t in by_weights))

    return step
```

profile of v0, /device:TPU:22, one launch (start us, length us, event | category | flops | bytes accessed | tf_op | source)
XLA Modules:
  0.0 583.4 jit_solution(13377397859733596874)
XLA Ops:
  22.7 27.5 %all-gather.29.cloned.1.call-done = bf16[1,512,1792]{2,1,0:T(8,128)(2,1)} async-done(((bf16[1,64,1792]{2,1,0:T(8,128)(2,1)}), bf16[1,512,1792]{2,1,0:T(8,128)(2,1)}) %all-gather.29.cloned.1.call-update) | async-done | bytes 1835024 | tf_op jit(solution)/vmap(jvp())/squeeze | solution.py:27
  50.2 8.8 %fusion.97 = f32[2048,1792]{1,0:T(8,128)} fusion(bf16[1,512,1792]{2,1,0:T(8,128)(2,1)} %all-gather.29.cloned.1.call-done, bf16[1,2048,512]{2,1,0:T(8,128)(2,1)S(1)} %copy-done.3, f32[2048]{0:T(1024)S(1)} %get-tuple-element.13), kind=kOutput, calls=%fused_computation.105 | convolution fusion | flops 3761242112 | bytes 18620416 | tf_op jit(solution)/vmap(jvp())/dot_general | solution.py:20
  59.0 28.5 %all-gather.31.cloned.1.call-done = bf16[1,512,1792]{2,1,0:T(8,128)(2,1)} async-done(((bf16[1,64,1792]{2,1,0:T(8,128)(2,1)}), bf16[1,512,1792]{2,1,0:T(8,128)(2,1)}) %all-gather.31.cloned.1.call-update) | async-done | bytes 1835024 | tf_op jit(solution)/vmap(jvp())/squeeze | solution.py:27
  87.5 5.7 fusion.94
  93.2 5.2 copy-done.1
  98.4 6.4 %fusion.24 = bf16[2048,1792]{1,0:T(8,128)(2,1)} fusion(f32[2048,1792]{1,0:T(8,128)S(1)} %fusion.94, f32[2048,1792]{1,0:T(8,128)S(1)} %copy-done), kind=kLoop, calls=%fused_computation.36 | loop fusion | flops 22020096 | bytes 36700160
  104.8 19.6 %all-gather.33.cloned.1.call-done = bf16[1,1792,512]{2,1,0:T(8,128)(2,1)} async-done(((bf16[1,224,512]{2,1,0:T(8,128)(2,1)}), bf16[1,1792,512]{2,1,0:T(8,128)(2,1)}) %all-gather.33.cloned.1.call-update) | async-done | bytes 1835024 | tf_op jit(solution)/vmap(jvp())/squeeze | solution.py:27
  124.4 9.3 %fusion.40 = (f32[2048]{0:T(1024)S(1)}, bf16[1,1,2048,512]{2,3,1,0:T(8,128)(2,1)}) fusion(bf16[2048,1792]{1,0:T(8,128)(2,1)} %fusion.24, bf16[1,1792,512]{2,1,0:T(8,128)(2,1)} %all-gather.33.cloned.1.call-done, bf16[1,2048,512]{1,2,0:T(8,128)(2,1)S(1)} %copy-done.4), kind=kOutput, calls=%fused_computation.62 | convolution fusion | flops 3763337216 | bytes 13377536 | tf_op jit(solution)/vmap(jvp())/dot_general | solution.py:9
  133.7 28.0 %all-gather.35.cloned.1.call-done = bf16[1,512,1792]{2,1,0:T(8,128)(2,1)} async-done(((bf16[1,64,1792]{2,1,0:T(8,128)(2,1)}), bf16[1,512,1792]{2,1,0:T(8,128)(2,1)}) %all-gather.35.cloned.1.call-update) | async-done | bytes 1835024 | tf_op jit(solution)/vmap(jvp())/squeeze | solution.py:27
  161.7 11.4 %fusion.89 = f32[2048,1792]{1,0:T(8,128)} fusion(bf16[1,512,1792]{2,1,0:T(8,128)(2,1)} %all-gather.35.cloned.1.call-done, bf16[1,1,2048,512]{2,3,1,0:T(8,128)(2,1)} %get-tuple-element.15, f32[2048]{0:T(1024)S(1)} %bitcast.308), kind=kOutput, calls=%fused_computation.97 | convolution fusion | flops 3761242112 | bytes 18620416 | tf_op jit(solution)/vmap(jvp())/dot_general | solution.py:20
  173.0 26.0 %all-gather.39.cloned.1.call-done = bf16[1,512,1792]{2,1,0:T(8,128)(2,1)} async-done(((bf16[1,64,1792]{2,1,0:T(8,128)(2,1)}), bf16[1,512,1792]{2,1,0:T(8,128)(2,1)}) %all-gather.39.cloned.1.call-update) | async-done | bytes 1835024 | tf_op jit(solution)/vmap(jvp())/squeeze | solution.py:27
  199.0 11.5 %fusion.84 = f32[2048,1792]{1,0:T(8,128)} fusion(bf16[1,512,1792]{2,1,0:T(8,128)(2,1)} %all-gather.39.cloned.1.call-done, bf16[1,1,2048,512]{2,3,1,0:T(8,128)(2,1)} %get-tuple-element.15, f32[2048]{0:T(1024)S(1)} %bitcast.309), kind=kOutput, calls=%fused_computation.92 | convolution fusion | flops 3761242112 | bytes 18620416 | tf_op jit(solution)/vmap(jvp())/dot_general | solution.py:21
  210.5 25.2 %all-gather.37.cloned.1.call-done = bf16[1,1792,512]{2,1,0:T(8,128)(2,1)} async-done(((bf16[1,224,512]{2,1,0:T(8,128)(2,1)}), bf16[1,1792,512]{2,1,0:T(8,128)(2,1)}) %all-gather.37.cloned.1.call-update) | async-done | bytes 1835024 | tf_op jit(solution)/vmap(jvp())/squeeze | solution.py:27
  235.7 7.8 %convolution_convert_fusion.1 = bf16[2048,1792]{1,0:T(8,128)(2,1)} fusion(bf16[1,2048,512]{2,1,0:T(8,128)(2,1)S(1)} %copy-done.9, bf16[1,1792,512]{2,1,0:T(8,128)(2,1)} %all-gather.37.cloned.1.call-done), kind=kOutput, calls=%fused_computation.35 | convolution fusion | flops 3761766400 | bytes 11272192 | tf_op jit(solution)/vmap(transpose(jvp()))/dot_general | solution.py:9
  243.5 10.4 %fusion.4 = bf16[2048,1792]{1,0:T(8,128)(2,1)S(1)} fusion(f32[2048,1792]{1,0:T(8,128)S(1)} %copy-done.2, f32[2048,1792]{1,0:T(8,128)} %fusion.84, bf16[2048,1792]{1,0:T(8,128)(2,1)} %convolution_convert_fusion.1), kind=kLoop, calls=%fused_computation.10 | loop fusion | flops 44040192 | bytes 44040192
  256.8 5.2 convolution_convert_fusion.3
  262.0 9.6 %fusion.42 = (f32[2048]{0:T(1024)S(1)}, bf16[1,1,2048,512]{2,3,1,0:T(8,128)(2,1)}) fusion(bf16[1,1,2048,512]{2,3,1,0:T(8,128)(2,1)S(1)} %copy-done.10, bf16[2048,512]{0,1:T(8,128)(2,1)} %convolution_convert_fusion.3, bf16[1,512,1792]{2,1,0:T(8,128)(2,1)} %all-gather.39.cloned.1.call-done, bf16[2048,1792]{1,0:T(8,128)(2,1)} %convolution_convert_fusion.1, ...), kind=kOutput, calls=%fused_computation.64 | convolution fusion | flops 3786405888 | bytes 30154752 | tf_op jit(solution)/vmap(transpose(jvp()))/dot_general | solution.py:21
  275.3 9.7 %convolution_bitcast_fusion.2 = f32[1,1792,512]{2,1,0:T(8,128)} fusion(bf16[2048,1792]{1,0:T(8,128)(2,1)} %fusion.24, bf16[1,1,2048,512]{2,3,1,0:T(8,128)(2,1)S(1)} %fusion.76), kind=kOutput, calls=%fused_computation.70 | convolution fusion | flops 3758096384 | bytes 13107200 | tf_op jit(solution)/vmap(transpose(jvp()))/dot_general | solution.py:9
  285.2 14.0 %fusion.43 = f32[1,1792,512]{2,1,0:T(8,128)} fusion(f32[2048,1792]{1,0:T(8,128)} %fusion.84, f32[2048,1792]{1,0:T(8,128)} %fusion.89, bf16[1,2048,512]{2,1,0:T(8,128)(2,1)} %param), kind=kOutput, calls=%fused_computation.65 | convolution fusion | flops 3780116480 | bytes 35127296 | tf_op jit(solution)/vmap(transpose(jvp()))/dot_general | solution.py:9
  299.4 8.1 %convolution_convert_fusion = bf16[2048,1792]{1,0:T(8,128)(2,1)} fusion(bf16[1,1,2048,512]{2,3,1,0:T(8,128)(2,1)S(1)} %fusion.76, bf16[1,1792,512]{2,1,0:T(8,128)(2,1)} %all-gather.33.cloned.1.call-done), kind=kOutput, calls=%fused_computation.34 | convolution fusion | flops 3761766400 | bytes 11272192 | tf_op jit(solution)/vmap(transpose(jvp()))/dot_general | solution.py:9
  307.4 16.5 %fusion.7 = bf16[2048,1792]{1,0:T(8,128)(2,1)} fusion(f32[2048,1792]{1,0:T(8,128)} %fusion.97, f32[2048,1792]{1,0:T(8,128)} %copy-done.1, bf16[2048,1792]{1,0:T(8,128)(2,1)} %convolution_convert_fusion), kind=kLoop, calls=%fused_computation.13 | loop fusion | flops 44040192 | bytes 44040192
  324.0 8.8 %fusion.46 = f32[1,512,1792]{2,1,0:T(8,128)} fusion(bf16[2048,1792]{1,0:T(8,128)(2,1)S(1)} %bitcast.303, f32[2048,1792]{1,0:T(8,128)S(1)} %bitcast.301, bf16[1,1,2048,512]{2,3,1,0:T(8,128)(2,1)} %get-tuple-element.15, f32[2048]{0:T(1024)S(1)} %bitcast.311), kind=kOutput, calls=%fused_computation.66 | convolution fusion | flops 3783262208 | bytes 27795456 | tf_op jit(solution)/vmap(transpose(jvp()))/dot_general | solution.py:21
  333.0 9.1 %convolution_convert_fusion.2 = bf16[2048,512]{0,1:T(8,128)(2,1)} fusion(bf16[2048,1792]{1,0:T(8,128)(2,1)} %fusion.7, bf16[1,512,1792]{2,1,0:T(8,128)(2,1)} %all-gather.29.cloned.1.call-done), kind=kOutput, calls=%fused_computation.73 | convolution fusion | flops 3758096384 | bytes 11272192 | tf_op jit(solution)/vmap(transpose(jvp()))/dot_general | solution.py:20
  342.1 14.8 %fusion.38 = (f32[2048]{0:T(1024)S(1)}, bf16[1,1,2048,512]{2,3,1,0:T(8,128)(2,1)}) fusion(bf16[1,2048,512]{1,2,0:T(8,128)(2,1)S(1)} %copy-done.5, bf16[2048,512]{0,1:T(8,128)(2,1)} %convolution_convert_fusion.2, bf16[1,512,1792]{2,1,0:T(8,128)(2,1)} %all-gather.31.cloned.1.call-done, bf16[2048,1792]{1,0:T(8,128)(2,1)} %convolution_convert_fusion, ...), kind=kOutput, calls=%fused_computation.60 | convolution fusion | flops 3786405888 | bytes 30154752 | tf_op jit(solution)/vmap(transpose(jvp()))/dot_general | solution.py:21
  357.0 9.3 %fusion.49 = f32[1,512,1792]{2,1,0:T(8,128)} fusion(bf16[2048,1792]{1,0:T(8,128)(2,1)} %convolution_convert_fusion, f32[2048,1792]{1,0:T(8,128)S(1)} %bitcast.299, bf16[1,2048,512]{1,2,0:T(8,128)(2,1)S(1)} %copy-done.5, f32[2048]{0:T(1024)S(1)} %bitcast.313), kind=kOutput, calls=%fused_computation.67 | convolution fusion | flops 3783262208 | bytes 27795456 | tf_op jit(solution)/vmap(transpose(jvp()))/dot_general | solution.py:21
  366.4 9.6 %convolution_bitcast_fusion.1 = f32[1,512,1792]{2,1,0:T(8,128)} fusion(bf16[2048,1792]{1,0:T(8,128)(2,1)} %copy-done.8, bf16[1,1,2048,512]{2,3,1,0:T(8,128)(2,1)} %get-tuple-element.15, f32[2048]{0:T(1024)S(1)} %bitcast.312), kind=kOutput, calls=%fused_computation.69 | convolution fusion | flops 3761242112 | bytes 13115392 | tf_op jit(solution)/vmap(transpose(jvp()))/dot_general | solution.py:20
  376.2 8.9 %convolution_bitcast_fusion = f32[1,512,1792]{2,1,0:T(8,128)} fusion(bf16[2048,1792]{1,0:T(8,128)(2,1)} %fusion.7, bf16[1,2048,512]{1,2,0:T(8,128)(2,1)S(1)} %copy-done.5, f32[2048]{0:T(1024)S(1)} %bitcast.314), kind=kOutput, calls=%fused_computation.68 | convolution fusion | flops 3761242112 | bytes 13115392 | tf_op jit(solution)/vmap(transpose(jvp()))/dot_general | solution.py:20
  385.2 4.9 fusion.75
  397.0 31.5 %reduce-scatter.23.cloned.1.call-done = f32[1,64,1792]{2,1,0:T(8,128)} async-done(((f32[1,512,1792]{2,1,0:T(8,128)}), f32[1,64,1792]{2,1,0:T(8,128)}) %reduce-scatter.23.cloned.1.call-update) | async-done | bytes 458768
  429.5 47.6 %reduce-scatter.25.cloned.1.call-done = f32[1,64,1792]{2,1,0:T(8,128)} async-done(((f32[1,512,1792]{2,1,0:T(8,128)}), f32[1,64,1792]{2,1,0:T(8,128)}) %reduce-scatter.25.cloned.1.call-update) | async-done | bytes 458768
  479.0 46.9 %reduce-scatter.19.cloned.1.call-done = f32[1,64,1792]{2,1,0:T(8,128)} async-done(((f32[1,512,1792]{2,1,0:T(8,128)}), f32[1,64,1792]{2,1,0:T(8,128)}) %reduce-scatter.19.cloned.1.call-update) | async-done | bytes 458768
  526.9 47.6 %reduce-scatter.21.cloned.1.call-done = f32[1,64,1792]{2,1,0:T(8,128)} async-done(((f32[1,512,1792]{2,1,0:T(8,128)}), f32[1,64,1792]{2,1,0:T(8,128)}) %reduce-scatter.21.cloned.1.call-update) | async-done | bytes 458768
  (96 shorter events, 35.5 us)
Async XLA Ops:
  7.2 8.1 %copy-start.3 = (bf16[1,2048,512]{2,1,0:T(8,128)(2,1)S(1)}, bf16[1,2048,512]{2,1,0:T(8,128)(2,1)}, u32[]{:S(2)}) copy-start(bf16[1,2048,512]{2,1,0:T(8,128)(2,1)} %param.1) | copy-start | bytes 6291460
  7.2 43.0 %all-gather.29.cloned.1.call-start = ((), (), s32[]{:S(2)}) async-start(), calls=%async_computation.6 | async-start | bytes 2064384 | tf_op jit(solution)/vmap(jvp())/squeeze | solution.py:27
  9.3 78.2 %all-gather.31.cloned.1.call-start = ((), (), s32[]{:S(2)}) async-start(), calls=%async_computation.7 | async-start | bytes 2064384 | tf_op jit(solution)/vmap(jvp())/squeeze | solution.py:27
  11.3 113.1 %all-gather.33.cloned.1.call-start = ((), (), s32[]{:S(2)}) async-start(), calls=%async_computation.8 | async-start | bytes 2064384 | tf_op jit(solution)/vmap(jvp())/squeeze | solution.py:27
  13.3 148.4 %all-gather.35.cloned.1.call-start = ((), (), s32[]{:S(2)}) async-start(), calls=%async_computation.9 | async-start | bytes 2064384 | tf_op jit(solution)/vmap(jvp())/squeeze | solution.py:27
  13.9 185.1 %all-gather.39.cloned.1.call-start = ((), (), s32[]{:S(2)}) async-start(), calls=%async_computation.11 | async-start | bytes 2064384 | tf_op jit(solution)/vmap(jvp())/squeeze | solution.py:27
  14.6 221.1 %all-gather.37.cloned.1.call-start = ((), (), s32[]{:S(2)}) async-start(), calls=%async_computation.10 | async-start | bytes 2064384 | tf_op jit(solution)/vmap(jvp())/squeeze | solution.py:27
  15.2 378.8 %reduce-scatter.29.cloned.1.call-start = ((), (), s32[]{:S(2)}) async-start(), calls=%async_computation.17 | async-start | bytes 4128768
  87.5 10.9 %copy-start = (f32[2048,1792]{1,0:T(8,128)S(1)}, f32[2048,1792]{1,0:T(8,128)}, u32[]{:S(2)}) copy-start(f32[2048,1792]{1,0:T(8,128)} %fusion.97) | copy-start | bytes 44040196
  98.4 26.0 %copy-start.4 = (bf16[1,2048,512]{1,2,0:T(8,128)(2,1)S(1)}, bf16[1,2048,512]{1,2,0:T(8,128)(2,1)}, u32[]{:S(2)}) copy-start(bf16[1,2048,512]{1,2,0:T(8,128)(2,1)} %copy.1) | copy-start | bytes 6291460
  173.0 62.7 %copy-start.9 = (bf16[1,2048,512]{2,1,0:T(8,128)(2,1)S(1)}, bf16[1,2048,512]{2,1,0:T(8,128)(2,1)}, u32[]{:S(2)}) copy-start(bf16[1,2048,512]{2,1,0:T(8,128)(2,1)} %param) | copy-start | bytes 6291460
  235.7 7.8 %copy-start.2 = (f32[2048,1792]{1,0:T(8,128)S(1)}, f32[2048,1792]{1,0:T(8,128)}, u32[]{:S(2)}) copy-start(f32[2048,1792]{1,0:T(8,128)} %fusion.89) | copy-start | bytes 44040196
  243.5 13.3 %copy-start.12 = (bf16[1,512,1792]{2,1,0:T(8,128)(2,1)S(1)}, bf16[1,512,1792]{2,1,0:T(8,128)(2,1)}, u32[]{:S(2)}) copy-start(bf16[1,512,1792]{2,1,0:T(8,128)(2,1)} %all-gather.35.cloned.1.call-done) | copy-start | bytes 5505028
  262.0 9.7 %copy-start.6 = (bf16[1,2048,512]{1,2,0:T(8,128)(2,1)S(1)}, bf16[1,2048,512]{1,2,0:T(8,128)(2,1)}, u32[]{:S(2)}) copy-start(bf16[1,2048,512]{1,2,0:T(8,128)(2,1)} %copy) | copy-start | bytes 6291460
  275.3 24.0 %copy-start.7 = (bf16[1,1,2048,512]{2,3,1,0:T(8,128)(2,1)}, bf16[1,1,2048,512]{2,3,1,0:T(8,128)(2,1)S(1)}, u32[]{:S(2)}) copy-start(bf16[1,1,2048,512]{2,3,1,0:T(8,128)(2,1)S(1)} %fusion.76) | copy-start | bytes 6291460
  285.1 110.0 %reduce-scatter.27.cloned.1.call-start = ((), (), s32[]{:S(2)}) async-start(), calls=%async_computation.16 | async-start | bytes 4128768
  299.3 129.2 %reduce-scatter.23.cloned.1.call-start = ((), (), s32[]{:S(2)}) async-start(), calls=%async_computation.14 | async-start | bytes 4128768
  299.4 24.6 %slice-start.4 = ((s8[14680064]{0:T(1024)(128)(4,1)}), s8[4194304]{0:T(1024)(128)(4,1)S(1)}, s32[]{:S(2)}) async-start(s8[14680064]{0:T(1024)(128)(4,1)} %bitcast.300), calls=%async_computation.22 | async-start | bytes 8388608
  299.4 24.6 %slice-start.5 = ((s8[14680064]{0:T(1024)(128)(4,1)}), s8[4194304]{0:T(1024)(128)(4,1)S(1)}, s32[]{:S(2)}) async-start(s8[14680064]{0:T(1024)(128)(4,1)} %bitcast.300), calls=%async_computation.23 | async-start | bytes 8388608
  299.4 24.6 %slice-start.8 = ((s8[7340032]{0:T(1024)(128)(4,1)}), s8[4194304]{0:T(1024)(128)(4,1)S(1)}, s32[]{:S(2)}) async-start(s8[7340032]{0:T(1024)(128)(4,1)} %bitcast.302), calls=%async_computation.26 | async-start | bytes 8388608
  307.4 16.6 %slice-start.6 = ((s8[14680064]{0:T(1024)(128)(4,1)}), s8[4194304]{0:T(1024)(128)(4,1)S(1)}, s32[]{:S(2)}) async-start(s8[14680064]{0:T(1024)(128)(4,1)} %bitcast.300), calls=%async_computation.24 | async-start | bytes 8388608
  307.4 16.6 %slice-start.7 = ((s8[14680064]{0:T(1024)(128)(4,1)}), s8[2097152]{0:T(1024)(128)(4,1)S(1)}, s32[]{:S(2)}) async-start(s8[14680064]{0:T(1024)(128)(4,1)} %bitcast.300), calls=%async_computation.25 | async-start | bytes 4194304
  307.4 16.6 %slice-start.9 = ((s8[7340032]{0:T(1024)(128)(4,1)}), s8[3145728]{0:T(1024)(128)(4,1)S(1)}, s32[]{:S(2)}) async-start(s8[7340032]{0:T(1024)(128)(4,1)} %bitcast.302), calls=%async_computation.27 | async-start | bytes 6291456
  332.9 9.2 %copy-start.5 = (bf16[1,2048,512]{1,2,0:T(8,128)(2,1)S(1)}, bf16[1,2048,512]{1,2,0:T(8,128)(2,1)}, u32[]{:S(2)}) copy-start(bf16[1,2048,512]{1,2,0:T(8,128)(2,1)} %copy.1) | copy-start | bytes 6291460
  332.9 144.2 %reduce-scatter.25.cloned.1.call-start = ((), (), s32[]{:S(2)}) async-start(), calls=%async_computation.15 | async-start | bytes 4128768
  333.0 24.0 %slice-start = ((s8[14680064]{0:T(1024)(128)(4,1)}), s8[4194304]{0:T(1024)(128)(4,1)S(1)}, s32[]{:S(2)}) async-start(s8[14680064]{0:T(1024)(128)(4,1)} %bitcast.298), calls=%async_computation.18 | async-start | bytes 8388608
  342.1 14.8 %copy-start.11 = (f32[2048]{0:T(1024)S(1)}, f32[2048]{0:T(1024)}, u32[]{:S(2)}) copy-start(f32[2048]{0:T(1024)} %get-tuple-element.12) | copy-start | bytes 24580
  342.1 14.9 %slice-start.1 = ((s8[14680064]{0:T(1024)(128)(4,1)}), s8[4194304]{0:T(1024)(128)(4,1)S(1)}, s32[]{:S(2)}) async-start(s8[14680064]{0:T(1024)(128)(4,1)} %bitcast.298), calls=%async_computation.19 | async-start | bytes 8388608
  342.1 14.9 %slice-start.2 = ((s8[14680064]{0:T(1024)(128)(4,1)}), s8[4194304]{0:T(1024)(128)(4,1)S(1)}, s32[]{:S(2)}) async-start(s8[14680064]{0:T(1024)(128)(4,1)} %bitcast.298), calls=%async_computation.20 | async-start | bytes 8388608
  342.1 14.9 %slice-start.3 = ((s8[14680064]{0:T(1024)(128)(4,1)}), s8[2097152]{0:T(1024)(128)(4,1)S(1)}, s32[]{:S(2)}) async-start(s8[14680064]{0:T(1024)(128)(4,1)} %bitcast.298), calls=%async_computation.21 | async-start | bytes 4194304
  366.3 159.6 %reduce-scatter.19.cloned.1.call-start = ((), (), s32[]{:S(2)}) async-start(), calls=%async_computation.12 | async-start | bytes 4128768
  376.0 198.5 %reduce-scatter.21.cloned.1.call-start = ((), (), s32[]{:S(2)}) async-start(), calls=%async_computation.13 | async-start | bytes 4128768
  (3 other events, 13.3 us)
Sparse Core Ops, SparseCore 0:
  9.6 40.5 all-gather.28
  52.3 35.1 all-gather.30
  89.1 35.2 all-gather.32
  126.4 35.2 all-gather.34
  163.7 35.2 all-gather.38
  200.4 35.2 all-gather.36
  285.3 45.6 reduce-scatter.28
  333.3 46.4 reduce-scatter.26
  382.1 46.3 reduce-scatter.22
  430.7 46.3 reduce-scatter.24
  479.5 46.3 reduce-scatter.18
  528.1 46.3 reduce-scatter.20
where the time goes:
time: 591 us; the launch traced here: 583 us
  waiting for transfers between devices  331 us (56%)
  matrix products  161 us (27%)
  other arithmetic  51.7 us (9%)
  local copies, waits for them, and re-layouts  24.1 us (4%)
  between operations  14.7 us (2%)
    unnamed x18, waiting for transfers between devices  176 us
    squeeze x6, waiting for transfers between devices, stack(): h = layer(h, {name: w[number] for name, w in weights.items()})  155 us
    dot_general x6, matrix products, layer(): up = jnp.dot(a, w['w_up'], preferred_element_type=jnp.float32)  59.7 us
    dot_general x6, matrix products, layer(): gate = jnp.dot(a, w['w_gate'], preferred_element_type=jnp.float32)  53 us
    dot_general x5, matrix products, matmul(): jnp.dot(a, w, preferred_element_type=jnp.float32).astype(jnp.bfloat16)  48.8 us
    unnamed x6, other arithmetic  33.3 us
    unnamed x49, local copies, waits for them, and re-layouts  18.4 us
  transfers between devices with their start and end apart: 12, of which 10 were waited for; matrix products, arithmetic and copies ran while one was open for 31% of the time, Pallas kernels for 0%

commit v1 on v0

v1 whole, which is shorter than its diff:
```python
import functools

import jax
import jax.numpy as jnp
from jax import lax
from jax.experimental import pallas as pl
from jax.experimental.pallas import tpu as pltpu
from jax.sharding import PartitionSpec as P

MESH = pl.DeviceIdType.MESH
F32, BF16 = jnp.float32, jnp.bfloat16
NN = (((1,), (0,)), ((), ()))
NT = (((1,), (1,)), ((), ()))


def dot(a, b, dims=NN):
    return lax.dot_general(a, b, dims, preferred_element_type=F32)


def chips_apart(mesh):
    first = mesh.devices.reshape(mesh.shape["rep"], -1)[:, 0]
    places = [getattr(d, "coords", None) for d in first]
    if places[0] is None:
        return 2, 4
    near = 2
    far = next((i for i, p in enumerate(places) if p[0] != places[0][0]), 4)
    return near, far


def kernel(cfg, x_hbm, dy_hbm, wp_hbm, dx_hbm, out_hbm,
           x, d, h, a, at, dt, acc, dgu, hid, w, g, ra, rb, out,
           zs, zr, xs, xr, cs, cr, rs, rr, local):
    n, near, far, tile, layers = cfg
    tokens, width = x.shape
    chunks, _, rows, _ = w.shape
    blocks = chunks // layers
    tall = width // n
    fb = width // 2
    quarter, half = width // 4, width // 2
    tiles = tokens // tile

    me, rep = lax.axis_index("dp"), lax.axis_index("rep")
    core, ybit, xbit = rep % 2, (rep // near) % 2, (rep // far) % 2
    other_core = rep + 1 - 2 * core
    other_y = rep + near * (1 - 2 * ybit)
    other_x = rep + far * (1 - 2 * xbit)

    def at_z(k):
        return lax.rem(me + k + 2 * n, n)

    barrier = pltpu.get_barrier_semaphore()
    for who in ({"dp": at_z(1)}, {"dp": at_z(-1)}, {"rep": other_core}, {"rep": other_y}, {"rep": other_x}):
        pl.semaphore_signal(barrier, inc=1, device_id=who, device_id_type=MESH)
    own = pltpu.make_async_copy(wp_hbm, w.at[:, me], local.at[0])
    own.start()
    get_x = pltpu.make_async_copy(x_hbm, x, local.at[1])
    get_x.start()
    get_d = pltpu.make_async_copy(dy_hbm, d, local.at[2])
    get_d.start()
    own.wait()
    pl.semaphore_wait(barrier, 5)

    def remote(src, dst, ssem, rsem, who):
        return pltpu.make_async_remote_copy(
            src_ref=src, dst_ref=dst, send_sem=ssem, recv_sem=rsem, device_id=who, device_id_type=MESH)

    def ag_chunk(c, k):
        par = c % 2
        s = 1 - 2 * par
        bit = ybit + par * (xbit - ybit)
        partner = other_y + par * (other_x - other_y)
        mine = pl.ds(pl.multiple_of((2 * core + bit) * quarter, quarter), quarter)
        theirs = pl.ds(pl.multiple_of((2 * core + 1 - bit) * quarter, quarter), quarter)
        mine2 = pl.ds(pl.multiple_of(core * half, half), half)
        theirs2 = pl.ds(pl.multiple_of((1 - core) * half, half), half)
        a_to, b_to = {"dp": at_z(s)}, {"dp": at_z(-s)}

        def hop(who, piece, m):
            ref = w.at[c, piece, :, mine]
            return remote(ref, ref, zs.at[c, m], zr.at[c, m], who)

        def across(piece, cols, m):
            ref = w.at[c, piece, :, cols]
            return remote(ref, ref, xs.at[c, m], xr.at[c, m], {"rep": partner})

        def within(piece, cols, m):
            ref = w.at[c, piece, :, cols]
            return remote(ref, ref, cs.at[c, m], cr.at[c, m], {"rep": other_core})

        def pieces(j):
            found = []
            if 1 <= j <= 4:
                found.append((at_z(-j * s), j - 1, a_to if j < 4 else None))
            if 1 <= j <= 3:
                found.append((at_z(j * s), 4 + j - 1, b_to if j < 3 else None))
            return found

        if k == 0:
            hop(a_to, me, 0).start()
            hop(b_to, me, 4).start()
        for piece, m, on in pieces(k):
            hop(a_to, piece, m).wait_recv()
            if on is not None:
                hop(on, piece, m + 1).start()
            across(piece, mine, m).start()
        for piece, m, _ in pieces(k - 1):
            across(piece, theirs, m).wait_recv()
            within(piece, mine2, m).start()
        for piece, m, _ in pieces(k - 2):
            within(piece, theirs2, m).wait_recv()

    def ag(i):
        for k in range(7):
            c = i - k
            if isinstance(c, int):
                if 0 <= c < chunks:
                    ag_chunk(jnp.int32(c), k)
            else:
                @pl.when(jnp.logical_and(c >= 0, c < chunks))
                def _(c=c, k=k):
                    ag_chunk(c, k)

    def rs_chunk(c, k):
        s = 1 - 2 * (c % 2)
        a_to, b_to = {"dp": at_z(s)}, {"dp": at_z(-s)}

        def send_a(src, m):
            return remote(src, ra.at[c, m], rs.at[c, m], rr.at[c, m], a_to)

        def send_b(src, m):
            return remote(src, rb.at[c, m], rs.at[c, 4 + m], rr.at[c, 4 + m], b_to)

        def add(ref, dest):
            ref[...] = (ref[...].astype(F32) + g[c, dest].astype(F32)).astype(BF16)

        if k == 0:
            send_a(g.at[c, at_z(4 * s)], 0).start()
        if k == 1:
            send_b(g.at[c, at_z(-3 * s)], 0).start()
        if 1 <= k <= 3:
            send_a(ra.at[c, k - 1], k - 1).wait_recv()
            add(ra.at[c, k - 1], at_z((4 - k) * s))
            send_a(ra.at[c, k - 1], k).start()
        if 2 <= k <= 3:
            send_b(rb.at[c, k - 2], k - 2).wait_recv()
            add(rb.at[c, k - 2], at_z(-(4 - k) * s))
            send_b(rb.at[c, k - 2], k - 1).start()
        if k == 4:
            send_a(ra.at[c, 3], 3).wait_recv()
            send_b(rb.at[c, 2], 2).wait_recv()
            out[c] = (g[c, me].astype(F32) + ra[c, 3].astype(F32) + rb[c, 2].astype(F32)).astype(BF16)

    def rs_step(i, first=0):
        for k in (3, 2, 1, 0, 4):
            if k < first:
                continue

            @pl.when(jnp.logical_and(i - k >= 0, i - k < chunks))
            def _(k=k):
                rs_chunk(chunk_at(i - k), k)

    def chunk_at(i):
        return jnp.where(i < blocks, i + (layers - 1) * blocks, i - blocks) if layers == 2 else i

    def over_tiles(body):
        def one(t, _):
            body(pl.ds(pl.multiple_of(t * tile, tile), tile))
            return 0
        lax.fori_loop(0, tiles, one, 0)

    def norm(src, with_t):
        def body(r):
            wide = src[r, :].astype(F32)
            scale = lax.rsqrt(jnp.mean(wide * wide, -1, keepdims=True) + 1e-6)
            normed = (wide * scale).astype(BF16)
            a[r, :] = normed
            acc[r, :] = jnp.zeros((tile, width), F32)
            if with_t:
                at[:, r] = normed.T
        over_tiles(body)

    def transpose_d():
        def body(r):
            dt[:, r] = d[r, :].T
        over_tiles(body)

    def forward_block(c):
        def body(r):
            gu = dot(a[r, :], w[c, :, :tall, :].reshape(width, width))
            gate, up = gu[:, :fb], gu[:, fb:]
            sig = 0.5 * jnp.tanh(0.5 * gate) + 0.5
            prod = (gate * sig * up).astype(BF16)
            acc[r, :] += dot(prod, w[c, :, tall:, :].reshape(fb, width))
        over_tiles(body)

    def backward_block(c):
        def body(r):
            wgu = w[c, :, :tall, :].reshape(width, width)
            gu = dot(a[r, :], wgu)
            dh = dot(d[r, :], w[c, :, tall:, :].reshape(fb, width), NT)
            gate, up = gu[:, :fb], gu[:, fb:]
            sig = 0.5 * jnp.tanh(0.5 * gate) + 0.5
            silu = gate * sig
            hid[r, :] = (silu * up).astype(BF16)
            dgu[r, fb:] = (dh * silu).astype(BF16)
            dgu[r, :fb] = (dh * up * (sig + silu * (1.0 - sig))).astype(BF16)
            acc[r, :] += dot(dgu[r, :], wgu, NT)
        over_tiles(body)
        g[c, :, :tall, :] = dot(at[...], dgu[...]).astype(BF16).reshape(n, tall, width)
        g[c, :, tall:, :] = dot(dt[...], hid[...]).T.astype(BF16).reshape(n, rows - tall, width)

    def norm_back(src, dst):
        def body(r):
            wide = src[r, :].astype(F32)
            scale = lax.rsqrt(jnp.mean(wide * wide, -1, keepdims=True) + 1e-6)
            da = acc[r, :]
            mix = jnp.mean(da * wide, -1, keepdims=True) * scale * scale
            dst[r, :] = (d[r, :].astype(F32) + scale * (da - wide * mix)).astype(BF16)
        over_tiles(body)

    ag(0)
    get_x.wait()
    ag(1)
    norm(x, False)
    get_d.wait()
    ag(2)
    transpose_d()
    for i in range(3, 7):
        ag(i)

    def fwd(j, _):
        forward_block(j)
        ag(j + 7)
        return 0
    lax.fori_loop(0, blocks, fwd, 0)

    def to_h(r):
        h[r, :] = (x[r, :].astype(F32) + acc[r, :].astype(BF16).astype(F32)).astype(BF16)
    over_tiles(to_h)
    norm(h, True)

    def bwd2(j, _):
        backward_block(j + blocks)
        rs_step(j)
        ag(j + 7 + blocks)
        return 0
    lax.fori_loop(0, blocks, bwd2, 0)

    norm_back(h, d)
    transpose_d()
    norm(x, True)

    def bwd1(j, _):
        backward_block(j)
        rs_step(j + blocks)
        return 0
    lax.fori_loop(0, blocks, bwd1, 0)

    norm_back(x, a)
    put_dx = pltpu.make_async_copy(a, dx_hbm, local.at[0])
    put_dx.start()

    def drain(i, _):
        rs_step(i, 1)
        return 0
    lax.fori_loop(chunks, chunks + 4, drain, 0)
    put_out = pltpu.make_async_copy(out, out_hbm, local.at[1])
    put_out.start()

    def sent(c, _):
        for m in range(7):
            q = w.at[c, 0, :, pl.ds(0, quarter)]
            remote(q, q, zs.at[c, m], zr.at[c, m], {"dp": at_z(1)}).wait_send()
            remote(q, q, xs.at[c, m], xr.at[c, m], {"dp": at_z(1)}).wait_send()
            q = w.at[c, 0, :, pl.ds(0, half)]
            remote(q, q, cs.at[c, m], cr.at[c, m], {"dp": at_z(1)}).wait_send()
            q = g.at[c, 0]
            remote(q, q, rs.at[c, m], rr.at[c, m], {"dp": at_z(1)}).wait_send()
        return 0
    lax.fori_loop(0, chunks, sent, 0)
    put_dx.wait()
    put_out.wait()


def solution(mesh):
    n = mesh.shape["dp"]
    near, far = chips_apart(mesh)

    def on_device(x, dy, wg, wu, wd):
        x, dy = x[0], dy[0]
        tokens, width = x.shape
        layers, tall, ff = wg.shape
        fb = width // 2
        blocks = ff // fb
        sub = fb // n
        rows = tall + sub
        chunks = layers * blocks
        tile = min(512, tokens)

        def cut(w):
            return w.reshape(layers, tall, n, blocks, sub).transpose(0, 3, 1, 2, 4).reshape(layers, blocks, tall, fb)

        wp = jnp.concatenate([cut(wg), cut(wu)], -1)
        wp = jnp.concatenate([wp, wd.reshape(layers, blocks, sub, width)], 2).reshape(chunks, rows, width)
        anywhere = pl.BlockSpec(memory_space=pl.ANY)
        dma = pltpu.SemaphoreType.DMA((chunks, 7))
        dx, out = pl.pallas_call(
            functools.partial(kernel, (n, near, far, tile, layers)),
            out_shape=(jax.ShapeDtypeStruct((tokens, width), BF16),
                       jax.ShapeDtypeStruct((chunks, rows, width), BF16)),
            in_specs=[anywhere] * 3,
            out_specs=(anywhere, anywhere),
            scratch_shapes=[
                pltpu.VMEM((tokens, width), BF16),
                pltpu.VMEM((tokens, width), BF16),
                pltpu.VMEM((tokens, width), BF16),
                pltpu.VMEM((tokens, width), BF16),
                pltpu.VMEM((width, tokens), BF16),
                pltpu.VMEM((width, tokens), BF16),
                pltpu.VMEM((tokens, width), F32),
                pltpu.VMEM((tokens, width), BF16),
                pltpu.VMEM((tokens, fb), BF16),
                pltpu.VMEM((chunks, n, rows, width), BF16),
                pltpu.VMEM((chunks, n, rows, width), BF16),
                pltpu.VMEM((chunks, 4, rows, width), BF16),
                pltpu.VMEM((chunks, 3, rows, width), BF16),
                pltpu.VMEM((chunks, rows, width), BF16),
                dma, dma, dma, dma, dma, dma, dma, dma,
                pltpu.SemaphoreType.DMA((3,)),
            ],
            compiler_params=pltpu.CompilerParams(
                collective_id=0, has_side_effects=True, vmem_limit_bytes=67_043_328),
        )(x, dy, wp)
        out = out.reshape(layers, blocks, rows, width)

        def whole(part):
            part = part.reshape(layers, blocks, tall, n, sub).transpose(0, 2, 3, 1, 4)
            return part.reshape(layers, tall, ff)

        return (dx[None], whole(out[:, :, :tall, :fb]), whole(out[:, :, :tall, fb:]),
                out[:, :, tall:, :].reshape(layers, blocks * sub, width))

    tokens_spec, w_spec = P(("rep", "dp"), None, None), P(None, "dp", None)
    return jax.shard_map(
        on_device, mesh=mesh,
        in_specs=(tokens_spec, tokens_spec, w_spec, w_spec, w_spec),
        out_specs=(tokens_spec, P("rep", "dp", None), P("rep", "dp", None), P("rep", "dp", None)),
        check_vma=False)
```

time: 591 us -> 202 us (0.34); the launches traced: 583 us -> 202 us
  waiting for transfers between devices: 331 us -> 0 us
  Pallas kernels: 0 us -> 188 us
  matrix products: 161 us -> 0 us
  other arithmetic: 51.7 us -> 1.21 us
  between operations: 14.7 us -> 0.74 us
  local copies, waits for them, and re-layouts: 24.1 us -> 12.1 us
    pallas_call x0 -> x1, Pallas kernels: none -> 188 us  [on_device(): pl.pallas_call(functools.partial(kernel, (n, near, far, tile, layers)), o...]
    unnamed x18 -> x0, waiting for transfers between devices: 176 us -> none
    dot_general x17 -> x0, matrix products: 161 us -> none  [the longest x6 59.7 us: layer(): up = jnp.dot(a, w['w_up'], preferred_element_type=jnp.float32)]
    squeeze x6 -> x0, waiting for transfers between devices: 155 us -> none  [stack(): h = layer(h, {name: w[number] for name, w in weights.items()})]
    unnamed x6 -> x0, other arithmetic: 33.3 us -> none
    unnamed x49 -> x11, local copies, waits for them, and re-layouts: 18.4 us -> 8.13 us
    reshape x4 -> x0, other arithmetic: 7.34 us -> none  [the longest x1 4.94 us: step(): by_x.reshape(shape)]
    broadcast_in_dim x6 -> x0, other arithmetic: 6.27 us -> none  [stack(): h = layer(h, {name: w[number] for name, w in weights.items()})]
  transfers between devices with their start and end apart: 12 -> 0, of which waited for: 10 -> 0; matrix products, arithmetic and copies ran while one was open for 31% -> 0% of each run, Pallas kernels for 0% -> 0%
where the time goes in v1:
time: 202 us
  Pallas kernels  188 us (93%)
  local copies, waits for them, and re-layouts  12.1 us (6%)
    pallas_call x1, Pallas kernels, on_device(): pl.pallas_call(functools.partial(kernel, (n, near, far, tile, layers)), o...  188 us
    unnamed x11, local copies, waits for them, and re-layouts  8.13 us

profile of v1, /device:TPU:22, one launch (start us, length us, event | category | flops | bytes accessed | tf_op | source)
XLA Modules:
  0.0 202.1 jit_solution(1464798788609254107)
XLA Ops:
  0.6 0.0 copy-start
  0.6 1.5 copy.13
  2.1 0.1 copy.14
  2.2 0.3 copy.17
  2.5 0.0 copy-done
  2.6 0.0 copy-start.1
  2.6 0.4 copy.15
  3.0 0.1 copy.16
  3.1 0.3 copy.18
  3.4 0.2 copy-done.1
  3.6 1.2 pad_maximum_fusion.wp_hbm
  4.8 188.0 %shard_map.84 = (bf16[2048,512]{1,0:T(8,128)(2,1)}, bf16[14,96,512]{2,1,0:T(8,128)(2,1)}) custom-call(bf16[2048,512]{1,0:T(8,128)(2,1)} %bitcast.30, bf16[2048,512]{1,0:T(8,128)(2,1)} %bitcast.31, bf16[14,96,512]{2,1,0:T(8,128)(2,1)} %pad_maximum_fusion.wp_hbm), custom_call_target="tpu_custom_call" | custom-call | tf_op jit(solution)/shard_map/pallas_call | solution.py:307
  192.8 1.8 slice.14
  194.7 1.2 fusion
  195.9 0.4 copy.26
  196.3 0.1 copy.22
  196.4 1.1 copy.24
  197.5 0.4 copy.25
  197.9 0.1 copy.20
  198.0 1.1 copy.23
  199.0 3.0 %copy.28 = bf16[1,2048,512]{2,1,0:T(8,128)(2,1)} copy(bf16[1,2048,512]{2,1,0:T(8,128)(2,1)} %bitcast.32) | data formatting | bytes 4194304
Async XLA Ops:
  0.6 1.9 copy-start
  2.6 1.0 copy-start.1

commit v2 on v1

v2 whole, which is shorter than its diff:
```python
import functools

import jax
import jax.numpy as jnp
from jax import lax
from jax.experimental import pallas as pl
from jax.experimental.pallas import tpu as pltpu
from jax.sharding import PartitionSpec as P

MESH = pl.DeviceIdType.MESH
F32, BF16 = jnp.float32, jnp.bfloat16
NN = (((1,), (0,)), ((), ()))
NT = (((1,), (1,)), ((), ()))
GAP, STAGES = 4, 7


def dot(a, b, dims=NN):
    return lax.dot_general(a, b, dims, preferred_element_type=F32)


def chips_apart(mesh):
    first = mesh.devices.reshape(mesh.shape["rep"], -1)[:, 0]
    places = [getattr(d, "coords", None) for d in first]
    if places[0] is None:
        return 2, 4
    near = 2
    far = next((i for i, p in enumerate(places) if p[0] != places[0][0]), 4)
    return near, far


def kernel(cfg, x_hbm, dy_hbm, wg_hbm, wu_hbm, wd_hbm, dx_hbm, og_hbm, ou_hbm, od_hbm,
           x, d, h, a1, at1, a2, at2, dt, acc, dgu, hid, wgs, wus, w, g, ra, rb, out,
           zs, zr, xs, xr, cs, cr, rs, rr, local):
    n, near, far, tile, layers = cfg
    tokens, width = x.shape
    chunks, _, rows, _ = w.shape
    blocks = chunks // layers
    tall = width // n
    fb = width // 2
    sub = fb // n
    quarter, half = width // 4, width // 2
    tiles = tokens // tile
    cut = rows // 2
    later = blocks - 1

    me, rep = lax.axis_index("dp"), lax.axis_index("rep")
    core, ybit, xbit = rep % 2, (rep // near) % 2, (rep // far) % 2
    other_core = rep + 1 - 2 * core
    other_y = rep + near * (1 - 2 * ybit)
    other_x = rep + far * (1 - 2 * xbit)

    def at_z(k):
        return lax.rem(me + k + 2 * n, n)

    barrier = pltpu.get_barrier_semaphore()
    for who in ({"dp": at_z(1)}, {"dp": at_z(-1)}, {"rep": other_core}, {"rep": other_y}, {"rep": other_x}):
        pl.semaphore_signal(barrier, inc=1, device_id=who, device_id_type=MESH)
    loads = [
        pltpu.make_async_copy(wg_hbm, wgs, local.at[0]),
        pltpu.make_async_copy(wu_hbm, wus, local.at[1]),
        pltpu.make_async_copy(wd_hbm, w.at[:, me, tall:, :], local.at[2]),
    ]
    get_x = pltpu.make_async_copy(x_hbm, x, local.at[3])
    get_d = pltpu.make_async_copy(dy_hbm, d, local.at[4])
    for copy in (*loads, get_x, get_d):
        copy.start()
    for copy in loads:
        copy.wait()

    def prepare(c):
        l, j = divmod(c, blocks)
        ff = sub * blocks
        parts = [src[l, :, o * ff + j * sub:o * ff + (j + 1) * sub] for src in (wgs, wus) for o in range(n)]
        w[c, me, :tall, :] = jnp.concatenate(parts, -1)

    def remote(src, dst, ssem, rsem, who):
        return pltpu.make_async_remote_copy(
            src_ref=src, dst_ref=dst, send_sem=ssem, recv_sem=rsem, device_id=who, device_id_type=MESH)

    def ag_chunk(c, k):
        par = c % 2
        s = 1 - 2 * par
        bit = ybit + par * (xbit - ybit)
        partner = other_y + par * (other_x - other_y)
        mine = pl.ds(pl.multiple_of((2 * core + bit) * quarter, quarter), quarter)
        theirs = pl.ds(pl.multiple_of((2 * core + 1 - bit) * quarter, quarter), quarter)
        mine2 = pl.ds(pl.multiple_of(core * half, half), half)
        theirs2 = pl.ds(pl.multiple_of((1 - core) * half, half), half)
        a_to, b_to = {"dp": at_z(s)}, {"dp": at_z(-s)}

        def hop(who, piece, m):
            ref = w.at[c, piece, :, mine]
            return remote(ref, ref, zs.at[c, m], zr.at[c, m], who)

        def across(piece, cols, m):
            ref = w.at[c, piece, :, cols]
            return remote(ref, ref, xs.at[c, m], xr.at[c, m], {"rep": partner})

        def within(piece, cols, m):
            ref = w.at[c, piece, :, cols]
            return remote(ref, ref, cs.at[c, m], cr.at[c, m], {"rep": other_core})

        def pieces(j):
            found = []
            if 1 <= j <= 4:
                found.append((at_z(-j * s), j - 1, a_to if j < 4 else None))
            if 1 <= j <= 3:
                found.append((at_z(j * s), 4 + j - 1, b_to if j < 3 else None))
            return found

        if k == 0:
            hop(a_to, me, 0).start()
            hop(b_to, me, 4).start()
        for piece, m, on in pieces(k):
            hop(a_to, piece, m).wait_recv()
            if on is not None:
                hop(on, piece, m + 1).start()
            across(piece, mine, m).start()
        for piece, m, _ in pieces(k - 1):
            across(piece, theirs, m).wait_recv()
            within(piece, mine2, m).start()
        for piece, m, _ in pieces(k - 2):
            within(piece, theirs2, m).wait_recv()

    def ag(i, first, gap):
        for k in range(STAGES - 1, -1, -1):
            c = i - gap * k
            if isinstance(c, int):
                if 0 <= c < blocks:
                    ag_chunk(jnp.int32(first + c), k)
            else:
                @pl.when(jnp.logical_and(c >= 0, c < blocks))
                def _(c=c, k=k):
                    ag_chunk(first + c, k)

    ag1 = functools.partial(ag, first=0, gap=GAP)
    ag2 = functools.partial(ag, first=blocks, gap=1)
    startup = GAP * (STAGES - 1)
    early = STAGES - (blocks + 1) // 2

    def rs_chunk(c, k):
        a_to, b_to = {"dp": at_z(1)}, {"dp": at_z(-1)}
        top, low = pl.ds(0, cut), pl.ds(cut, cut)

        def send_a(src, dst, m):
            return remote(src, dst, rs.at[c, m], rr.at[c, m], a_to)

        def send_b(src, dst, m):
            return remote(src, dst, rs.at[c, 4 + m], rr.at[c, 4 + m], b_to)

        def add(ref, dest, part):
            ref[part, :] = (ref[part, :].astype(F32) + g[c, dest, part, :].astype(F32)).astype(BF16)

        everything = pl.ds(0, rows)
        if k == 0:
            send_a(g.at[c, at_z(4), top], ra.at[c, 0, top], 0).start()
            send_b(g.at[c, at_z(-4), low], rb.at[c, 0, low], 0).start()
        if k == 1:
            ra[c, 0, low, :] = g[c, at_z(3), low, :]
            rb[c, 0, top, :] = g[c, at_z(-3), top, :]
            send_a(ra.at[c, 0, top], ra.at[c, 0, top], 0).wait_recv()
            add(ra.at[c, 0], at_z(3), top)
            send_a(ra.at[c, 0], ra.at[c, 1], 1).start()
            send_b(rb.at[c, 0, low], rb.at[c, 0, low], 0).wait_recv()
            add(rb.at[c, 0], at_z(-3), low)
            send_b(rb.at[c, 0], rb.at[c, 1], 1).start()
        if k in (2, 3):
            send_a(ra.at[c, k - 1], ra.at[c, k - 1], k - 1).wait_recv()
            add(ra.at[c, k - 1], at_z(4 - k), everything)
            send_a(ra.at[c, k - 1], ra.at[c, k], k).start()
            send_b(rb.at[c, k - 1], rb.at[c, k - 1], k - 1).wait_recv()
            add(rb.at[c, k - 1], at_z(k - 4), everything)
            send_b(rb.at[c, k - 1], rb.at[c, k], k).start()
        if k == 4:
            send_a(ra.at[c, 3], ra.at[c, 3], 3).wait_recv()
            send_b(rb.at[c, 3], rb.at[c, 3], 3).wait_recv()
            out[c] = (g[c, me].astype(F32) + ra[c, 3].astype(F32) + rb[c, 3].astype(F32)).astype(BF16)

    def chunk_at(i):
        return lax.rem(i + (layers - 1) * blocks, chunks)

    def rs_do(i, k):
        @pl.when(jnp.logical_and(i - k >= 0, i - k < chunks))
        def _():
            rs_chunk(chunk_at(i - k), k)

    def over_tiles(body, between=None):
        def one(t, _):
            if between is not None:
                between(t)
            body(pl.ds(pl.multiple_of(t * tile, tile), tile))
            return 0
        lax.fori_loop(0, tiles, one, 0)

    def put_normed(wide, r, a, at):
        scale = lax.rsqrt(jnp.mean(wide * wide, -1, keepdims=True) + 1e-6)
        normed = (wide * scale).astype(BF16)
        a[r, :] = normed
        at[:, r] = normed.T

    def first_norm():
        def body(r):
            put_normed(x[r, :].astype(F32), r, a1, at1)
            acc[r, :] = jnp.zeros((tile, width), F32)
        over_tiles(body)

    def transpose_d():
        def body(r):
            dt[:, r] = d[r, :].T
        over_tiles(body)

    def next_state():
        def body(r):
            new = (x[r, :].astype(F32) + acc[r, :].astype(BF16).astype(F32)).astype(BF16)
            h[r, :] = new
            put_normed(new.astype(F32), r, a2, at2)
            acc[r, :] = jnp.zeros((tile, width), F32)
        over_tiles(body)

    def forward_block(c, between):
        def body(r):
            gu = dot(a1[r, :], w[c, :, :tall, :].reshape(width, width))
            gate, up = gu[:, :fb], gu[:, fb:]
            sig = 0.5 * jnp.tanh(0.5 * gate) + 0.5
            prod = (gate * sig * up).astype(BF16)
            acc[r, :] += dot(prod, w[c, :, tall:, :].reshape(fb, width))
        over_tiles(body, between)

    def backward_block(c, a, at, between, after):
        def body(r):
            wgu = w[c, :, :tall, :].reshape(width, width)
            gu = dot(a[r, :], wgu)
            dh = dot(d[r, :], w[c, :, tall:, :].reshape(fb, width), NT)
            gate, up = gu[:, :fb], gu[:, fb:]
            sig = 0.5 * jnp.tanh(0.5 * gate) + 0.5
            silu = gate * sig
            hid[r, :] = (silu * up).astype(BF16)
            dgu[r, fb:] = (dh * silu).astype(BF16)
            dgu[r, :fb] = (dh * up * (sig + silu * (1.0 - sig))).astype(BF16)
            acc[r, :] += dot(dgu[r, :], wgu, NT)
        over_tiles(body, between)
        after()
        g[c, :, :tall, :] = dot(at[...], dgu[...]).astype(BF16).reshape(n, tall, width)
        g[c, :, tall:, :] = dot(dt[...], hid[...]).T.astype(BF16).reshape(n, rows - tall, width)

    def norm_back(src, dst, last):
        def body(r):
            wide = src[r, :].astype(F32)
            scale = lax.rsqrt(jnp.mean(wide * wide, -1, keepdims=True) + 1e-6)
            da = acc[r, :]
            mix = jnp.mean(da * wide, -1, keepdims=True) * scale * scale
            new = (d[r, :].astype(F32) + scale * (da - wide * mix)).astype(BF16)
            dst[r, :] = new
            if not last:
                dt[:, r] = new.T
                acc[r, :] = jnp.zeros((tile, width), F32)
        over_tiles(body)

    prepare(0)
    pl.semaphore_wait(barrier, 5)
    for i in range(startup + 1):
        ag1(i)
        if i + 1 < chunks:
            prepare(i + 1)
        if i == blocks:
            get_x.wait()
            first_norm()
        if i == blocks + GAP:
            get_d.wait()
            transpose_d()
        q = early - 1 - (startup - 2 - i) // 4
        if (startup - 2 - i) % 4 == 0 and 0 <= q < early:
            ag2(q)

    def fwd(j, _):
        def between(t):
            for m in range(2):
                @pl.when(t == m * tiles // 2)
                def _():
                    ag1(startup + 1 + 2 * j + m)

            @pl.when(jnp.logical_and(t == tiles - 1, j % 2 == 0))
            def _():
                ag2(early + j // 2)
        forward_block(j, between)
        return 0
    lax.fori_loop(0, blocks, fwd, 0)
    next_state()

    def rs_between(i):
        def between(t):
            for m in range(3):
                @pl.when(t == m * tiles // 4)
                def _():
                    rs_do(i, 4 - m)
        return between

    def bwd2(j, _):
        backward_block(j + blocks, a2, at2, rs_between(j), lambda: rs_do(j, 1))
        rs_do(j, 0)
        ag2(STAGES + j)
        return 0
    lax.fori_loop(0, blocks, bwd2, 0)

    norm_back(h, d, False)

    def bwd1(j, _):
        backward_block(j, a1, at1, rs_between(j + blocks), lambda: rs_do(j + blocks, 1))
        rs_do(j + blocks, 0)
        return 0
    lax.fori_loop(0, blocks, bwd1, 0)

    norm_back(x, a2, True)
    put_dx = pltpu.make_async_copy(a2, dx_hbm, local.at[0])
    put_dx.start()

    def drain(i, _):
        for k in (3, 2, 1, 4):
            rs_do(i, k)
        return 0

    def put_out(l, at):
        blocks_of = pl.ds(l * blocks, blocks)
        for which, dst in enumerate((wgs, wus)):
            dst[l] = jnp.concatenate(
                [out[l * blocks + j, :tall, which * fb + o * sub:which * fb + (o + 1) * sub]
                 for o in range(n) for j in range(blocks)], -1)
        return [pltpu.make_async_copy(out.at[blocks_of, tall:, :], od_hbm.at[blocks_of], local.at[at]),
                pltpu.make_async_copy(wgs.at[l], og_hbm.at[l], local.at[at + 1]),
                pltpu.make_async_copy(wus.at[l], ou_hbm.at[l], local.at[at + 2])]

    def gathers_sent(c, _):
        for m in range(7):
            q = w.at[c, 0, :, pl.ds(0, quarter)]
            remote(q, q, zs.at[c, m], zr.at[c, m], {"dp": at_z(1)}).wait_send()
            remote(q, q, xs.at[c, m], xr.at[c, m], {"dp": at_z(1)}).wait_send()
            q = w.at[c, 0, :, pl.ds(0, half)]
            remote(q, q, cs.at[c, m], cr.at[c, m], {"dp": at_z(1)}).wait_send()
        return 0

    def sums_sent(c, _):
        for m in range(8):
            q = g.at[c, 0, pl.ds(0, cut)] if m % 4 == 0 else g.at[c, 0]
            remote(q, q, rs.at[c, m], rr.at[c, m], {"dp": at_z(1)}).wait_send()
        return 0

    lax.fori_loop(chunks, chunks + 1, drain, 0)
    puts = []
    for l in range(1, layers):
        puts += put_out(l, 3 * l + 1)
    for copy in puts:
        copy.start()
    lax.fori_loop(0, chunks, gathers_sent, 0)
    lax.fori_loop(chunks + 1, chunks + 4, drain, 0)
    last = put_out(0, 1)
    for copy in last:
        copy.start()
    lax.fori_loop(0, chunks, sums_sent, 0)
    for copy in (put_dx, *puts, *last):
        copy.wait()


def handed_on(*arrays):
    pieces = [(i, k) for i, a in enumerate(arrays) for k in range(4 if i == 0 else 1)]

    def body(*refs):
        src, dst = refs[:len(arrays)], refs[len(arrays):2 * len(arrays)]
        here, sems = refs[2 * len(arrays):3 * len(arrays)], refs[-1]

        def part(ref, i, k):
            if i:
                return ref
            rows = ref.shape[0] // 4
            return ref.at[pl.ds(k * rows, rows)]

        into = [pltpu.make_async_copy(part(src[i], i, k), part(here[i], i, k), sems.at[0, m])
                for m, (i, k) in enumerate(pieces)]
        back = [pltpu.make_async_copy(part(here[i], i, k), part(dst[i], i, k), sems.at[1, m])
                for m, (i, k) in enumerate(pieces)]
        for copy in into:
            copy.start()
        for one, two in zip(into, back):
            one.wait()
            two.start()
        for copy in back:
            copy.wait()

    anywhere = pl.BlockSpec(memory_space=pl.ANY)
    return pl.pallas_call(
        body,
        out_shape=tuple(jax.ShapeDtypeStruct(a.shape, a.dtype) for a in arrays),
        in_specs=[anywhere] * len(arrays),
        out_specs=(anywhere,) * len(arrays),
        scratch_shapes=[*(pltpu.VMEM(a.shape, a.dtype) for a in arrays),
                        pltpu.SemaphoreType.DMA((2, len(pieces)))],
    )(*arrays)


def solution(mesh):
    n = mesh.shape["dp"]
    near, far = chips_apart(mesh)

    def on_device(x, dy, wg, wu, wd):
        x, dy = x[0], dy[0]
        tokens, width = x.shape
        layers, tall, ff = wg.shape
        fb = width // 2
        blocks = ff // fb
        sub = fb // n
        rows = tall + sub
        chunks = layers * blocks
        tile = min(1024, tokens // 2)
        anywhere = pl.BlockSpec(memory_space=pl.ANY)
        seven, eight = pltpu.SemaphoreType.DMA((chunks, 7)), pltpu.SemaphoreType.DMA((chunks, 8))
        wide, high = pltpu.VMEM((tokens, width), BF16), pltpu.VMEM((width, tokens), BF16)
        dx, og, ou, od = pl.pallas_call(
            functools.partial(kernel, (n, near, far, tile, layers)),
            out_shape=(jax.ShapeDtypeStruct(x.shape, BF16),
                       jax.ShapeDtypeStruct(wg.shape, BF16),
                       jax.ShapeDtypeStruct(wu.shape, BF16),
                       jax.ShapeDtypeStruct((chunks, sub, width), BF16)),
            in_specs=[anywhere] * 5,
            out_specs=(anywhere,) * 4,
            scratch_shapes=[
                wide, wide, wide, wide, high, wide, high, high,
                pltpu.VMEM((tokens, width), F32),
                wide,
                pltpu.VMEM((tokens, fb), BF16),
                pltpu.VMEM(wg.shape, BF16),
                pltpu.VMEM(wu.shape, BF16),
                pltpu.VMEM((chunks, n, rows, width), BF16),
                pltpu.VMEM((chunks, n, rows, width), BF16),
                pltpu.VMEM((chunks, 4, rows, width), BF16),
                pltpu.VMEM((chunks, 4, rows, width), BF16),
                pltpu.VMEM((chunks, rows, width), BF16),
                seven, seven, seven, seven, seven, seven, eight, eight,
                pltpu.SemaphoreType.DMA((7,)),
            ],
            compiler_params=pltpu.CompilerParams(
                collective_id=0, has_side_effects=True, vmem_limit_bytes=67_043_328),
        )(x, dy, wg, wu, wd.reshape(chunks, sub, width))
        dx, og, ou, od = handed_on(dx, og, ou, od)
        return dx[None], og, ou, od.reshape(wd.shape)

    tokens_spec, w_spec = P(("rep", "dp"), None, None), P(None, "dp", None)
    return jax.shard_map(
        on_device, mesh=mesh,
        in_specs=(tokens_spec, tokens_spec, w_spec, w_spec, w_spec),
        out_specs=(tokens_spec, P("rep", "dp", None), P("rep", "dp", None), P("rep", "dp", None)),
        check_vma=False)
```

time: 202 us -> 179 us (0.89)
  local copies, waits for them, and re-layouts: 12.1 us -> 0 us
  Pallas kernels: 188 us -> 178 us
    pallas_call x1, Pallas kernels: 188 us -> 176 us  [on_device(): pl.pallas_call(functools.partial(kernel, (n, near, far, tile, layers)), o...]
    unnamed x11 -> x0, local copies, waits for them, and re-layouts: 8.13 us -> none
    slice x2 -> x0, local copies, waits for them, and re-layouts: 3.06 us -> none  [the longest x1 1.83 us: on_device(): out[:, :, tall:, :].reshape(layers, blocks * sub, width)]
    pallas_call x0 -> x1, Pallas kernels: none -> 2.92 us  [handed_on(): pl.pallas_call(body, out_shape=tuple((jax.ShapeDtypeStruct(a.shape, a.dty...]
where the time goes in v2:
time: 179 us
  Pallas kernels  178 us (99%)
    pallas_call x1, Pallas kernels, on_device(): pl.pallas_call(functools.partial(kernel, (n, near, far, tile, layers)), o...  176 us

profile of v2, /device:TPU:22, one launch (start us, length us, event | category | flops | bytes accessed | tf_op | source)
XLA Modules:
  0.0 179.3 jit_solution(7771077523134842970)
XLA Ops:
  0.6 175.5 %shard_map.84 = (bf16[2048,512]{1,0:T(8,128)(2,1)}, bf16[2,64,1792]{2,1,0:T(8,128)(2,1)}, bf16[2,64,1792]{2,1,0:T(8,128)(2,1)}, bf16[14,32,512]{2,1,0:T(8,128)(2,1)}) custom-call(bf16[2048,512]{1,0:T(8,128)(2,1)} %bitcast.5, bf16[2048,512]{1,0:T(8,128)(2,1)} %bitcast.6, bf16[2,64,1792]{2,1,0:T(8,128)(2,1)} %wg_hbm.1, bf16[2,64,1792]{2,1,0:T(8,128)(2,1)} %wu_hbm.1, ...), custom_call_target="tpu_custom_call" | custom-call | tf_op jit(solution)/shard_map/pallas_call | solution.py:416
  176.2 2.9 %shard_map.85 = (bf16[2048,512]{1,0:T(8,128)(2,1)}, bf16[2,64,1792]{2,1,0:T(8,128)(2,1)}, bf16[2,64,1792]{2,1,0:T(8,128)(2,1)}, bf16[14,32,512]{2,1,0:T(8,128)(2,1)}) custom-call(bf16[2048,512]{1,0:T(8,128)(2,1)} %get-tuple-element.12.refs_0_, bf16[2,64,1792]{2,1,0:T(8,128)(2,1)} %get-tuple-element.13.refs_1_, ...), custom_call_target="tpu_custom_call" | custom-call | tf_op jit(solution)/shard_map/pallas_call | solution.py:389

commit v3 on v2

--- a/solution.py
+++ b/solution.py
@@ -243,7 +243,7 @@
         g[c, :, :tall, :] = dot(at[...], dgu[...]).astype(BF16).reshape(n, tall, width)
         g[c, :, tall:, :] = dot(dt[...], hid[...]).T.astype(BF16).reshape(n, rows - tall, width)
 
-    def norm_back(src, dst, last):
+    def norm_back(src, dst, last, between):
         def body(r):
             wide = src[r, :].astype(F32)
             scale = lax.rsqrt(jnp.mean(wide * wide, -1, keepdims=True) + 1e-6)
@@ -254,7 +254,7 @@
             if not last:
                 dt[:, r] = new.T
                 acc[r, :] = jnp.zeros((tile, width), F32)
-        over_tiles(body)
+        over_tiles(body, between)
 
     prepare(0)
     pl.semaphore_wait(barrier, 5)
@@ -274,25 +274,37 @@
 
     def fwd(j, _):
         def between(t):
-            for m in range(2):
+            @pl.when(t == tiles // 2)
+            def _():
+                ag1(startup + 1 + 2 * j)
+        forward_block(j, between)
+        ag1(startup + 2 + 2 * j)
+
+        @pl.when(j % 2 == 0)
+        def _():
+            ag2(early + j // 2)
+        return 0
+    lax.fori_loop(0, blocks, fwd, 0)
+    next_state()
+
+    def rs_between(i):
+        def between(t):
+            @pl.when(jnp.logical_and(t == 0, i != blocks))
+            def _():
+                rs_do(i, 4)
+                rs_do(i, 3)
+
+            @pl.when(t == tiles // 2)
+            def _():
+                rs_do(i, 2)
+        return between
+
+    def rs_halves(i, ks):
+        def between(t):
+            for m, k in enumerate(ks):
                 @pl.when(t == m * tiles // 2)
                 def _():
-                    ag1(startup + 1 + 2 * j + m)
-
-            @pl.when(jnp.logical_and(t == tiles - 1, j % 2 == 0))
-            def _():
-                ag2(early + j // 2)
-        forward_block(j, between)
-        return 0
-    lax.fori_loop(0, blocks, fwd, 0)
-    next_state()
-
-    def rs_between(i):
-        def between(t):
-            for m in range(3):
-                @pl.when(t == m * tiles // 4)
-                def _():
-                    rs_do(i, 4 - m)
+                    rs_do(jnp.int32(i), k)
         return between
 
     def bwd2(j, _):
@@ -302,7 +314,7 @@
         return 0
     lax.fori_loop(0, blocks, bwd2, 0)
 
-    norm_back(h, d, False)
+    norm_back(h, d, False, rs_halves(blocks, (4, 3)))
 
     def bwd1(j, _):
         backward_block(j, a1, at1, rs_between(j + blocks), lambda: rs_do(j + blocks, 1))
@@ -310,7 +322,7 @@
         return 0
     lax.fori_loop(0, blocks, bwd1, 0)
 
-    norm_back(x, a2, True)
+    norm_back(x, a2, True, rs_halves(chunks, (3, 2)))
     put_dx = pltpu.make_async_copy(a2, dx_hbm, local.at[0])
     put_dx.start()
 
@@ -344,7 +356,8 @@
             remote(q, q, rs.at[c, m], rr.at[c, m], {"dp": at_z(1)}).wait_send()
         return 0
 
-    lax.fori_loop(chunks, chunks + 1, drain, 0)
+    for k in (1, 4):
+        rs_do(jnp.int32(chunks), k)
     puts = []
     for l in range(1, layers):
         puts += put_out(l, 3 * l + 1)

time: 179 us -> 178 us (level)
  no operation moved by 1% of the time
where the time goes in v3:
time: 178 us
  Pallas kernels  177 us (99%)
    pallas_call x1, Pallas kernels, on_device(): pl.pallas_call(functools.partial(kernel, (n, near, far, tile, layers)), o...  174 us

profile of v3, /device:TPU:22, one launch (start us, length us, event | category | flops | bytes accessed | tf_op | source)
XLA Modules:
  0.0 178.2 jit_solution(15109768733377702466)
XLA Ops:
  0.6 174.5 %shard_map.84 = (bf16[2048,512]{1,0:T(8,128)(2,1)}, bf16[2,64,1792]{2,1,0:T(8,128)(2,1)}, bf16[2,64,1792]{2,1,0:T(8,128)(2,1)}, bf16[14,32,512]{2,1,0:T(8,128)(2,1)}) custom-call(bf16[2048,512]{1,0:T(8,128)(2,1)} %bitcast.5, bf16[2048,512]{1,0:T(8,128)(2,1)} %bitcast.6, bf16[2,64,1792]{2,1,0:T(8,128)(2,1)} %wg_hbm.1, bf16[2,64,1792]{2,1,0:T(8,128)(2,1)} %wu_hbm.1, ...), custom_call_target="tpu_custom_call" | custom-call | tf_op jit(solution)/shard_map/pallas_call | solution.py:429
  175.1 2.9 %shard_map.85 = (bf16[2048,512]{1,0:T(8,128)(2,1)}, bf16[2,64,1792]{2,1,0:T(8,128)(2,1)}, bf16[2,64,1792]{2,1,0:T(8,128)(2,1)}, bf16[14,32,512]{2,1,0:T(8,128)(2,1)}) custom-call(bf16[2048,512]{1,0:T(8,128)(2,1)} %get-tuple-element.12.refs_0_, bf16[2,64,1792]{2,1,0:T(8,128)(2,1)} %get-tuple-element.13.refs_1_, ...), custom_call_target="tpu_custom_call" | custom-call | tf_op jit(solution)/shard_map/pallas_call | solution.py:402
